TPU v7x, 32 devices: a whole 2x2x4 slice. The times are simulated.
32 devices in a mesh: ctx: 8 (over z, x), tp: 4 (over y, core).
Axes of the slice: x: 2, y: 2, z: 4, core: 2. Of those that a mesh axis runs over, the one named last changes fastest.
Arguments:
- query_plain: bfloat16 [1024, 8192], P('ctx', 'tp'), may hold values from -6 to 6
- query_rotary: bfloat16 [1024, 4096], P('ctx', 'tp'), may hold values from -6 to 6
- latent_keys: bfloat16 [1024, 576], P(('ctx', 'tp')), may hold values from -100 to 100
- span_order: int32 [16], replicated, may hold values from 0 to 15, each once
- key_up: bfloat16 [64, 128, 512], P('tp'), may hold values from -0.5 to 0.5
- value_up: bfloat16 [64, 512, 128], P('tp'), may hold values from -0.5 to 0.5
- output_weight: bfloat16 [8192, 3584], P('tp'), may hold values from -0.125 to 0.125
Outputs:
- mixed: bfloat16 [1024, 3584], P('ctx', 'tp')
Inputs may be any that keep to these rules, and one draw needn't show every extreme that they name: Stored rows s * 64 to (s + 1) * 64 - 1 are the tokens of span span_order[s] of the sequence, in order; each span appears once.
All inputs are finite; a program needn't handle non-finite values.
Results may differ from a plain program's by a relative error of at most 0.015.
Values may be sent and summed in bfloat16 or wider, within the bound.
A program may use at most 64 MiB of HBM per device.

v0:
```python
import math
from functools import partial

import jax
import jax.numpy as jnp
from jax import lax
from jax.experimental import pallas as pl
from jax.experimental.pallas import tpu as pltpu
from jax.sharding import PartitionSpec as P

rope_base = 10000.0
fill_score = -1e30
key_block_rows = 512


def rotate_pairs(values, places):
    halfway = values.shape[-1] // 2
    frequency = rope_base ** (-jnp.arange(halfway, dtype=jnp.float32) * 2.0 / values.shape[-1])
    angles = places.astype(jnp.float32)[:, None] * frequency[None, :]
    cosine = jnp.cos(angles)
    sine_part = jnp.sin(angles)
    if values.ndim == 3:
        cosine = cosine[:, None, :]
        sine_part = sine_part[:, None, :]
    first_half = values[..., :halfway]
    second_half = values[..., halfway:]
    return jnp.concatenate(
        [
            first_half * cosine - second_half * sine_part,
            first_half * sine_part + second_half * cosine,
        ],
        axis=-1,
    )


def token_places(span_table, indices, span_len):
    slot_ids = indices // span_len
    slot_table = jnp.arange(span_table.shape[0], dtype=jnp.int32)
    picked = jnp.sum(
        jnp.where(slot_ids[:, None] == slot_table[None, :], span_table[None, :], 0), axis=1
    )
    return picked * span_len + indices % span_len


def attend_block(
    carry_state, keys_block, key_places, queries, query_places, latent_width, score_scale
):
    running_max, running_sum, summed = carry_state
    scores = jnp.dot(queries, keys_block.T, preferred_element_type=jnp.float32) * score_scale
    allowed = key_places[None, :] <= query_places[:, None]
    masked = jnp.where(allowed, scores, fill_score)
    new_max = jnp.maximum(running_max, jnp.max(masked, axis=1))
    weights = jnp.where(allowed, jnp.exp(scores - new_max[:, None]), 0.0)
    factor = jnp.exp(running_max - new_max)
    new_sum = running_sum * factor + jnp.sum(weights, axis=1)
    new_summed = summed * factor[:, None] + jnp.dot(
        weights.astype(jnp.bfloat16),
        keys_block[:, :latent_width],
        preferred_element_type=jnp.float32,
    )
    return (new_max, new_sum, new_summed)


def attend_guarded(
    carry_state, keys_block, key_places, queries, query_places, latest, latent_width, score_scale
):
    return lax.cond(
        jnp.min(key_places) > latest,
        lambda carried: carried,
        lambda carried: attend_block(
            carried, keys_block, key_places, queries, query_places, latent_width, score_scale
        ),
        carry_state,
    )


def make_folder(queries, row_places, latest, span_order, span_len, latent_width, score_scale):

    def fold_piece(carry_state, key_piece, offset):
        piece_rows = key_piece.shape[0]
        key_places = token_places(span_order, jnp.arange(piece_rows, dtype=jnp.int32), span_len)

        def step_block(carried, block_parts):
            return (
                attend_guarded(
                    carried,
                    block_parts[0],
                    block_parts[1],
                    queries,
                    row_places,
                    latest,
                    latent_width,
                    score_scale,
                ),
                None,
            )

        stacked = key_piece.reshape(
            piece_rows // key_block_rows, key_block_rows, key_piece.shape[1]
        )
        stacked_places = key_places.reshape(piece_rows // key_block_rows, key_block_rows)
        result_state, unused = lax.scan(step_block, carry_state, (stacked, stacked_places))
        return result_state

    return fold_piece


def start_state(row_count, latent_width):
    return (
        jnp.full((row_count,), fill_score, jnp.float32),
        jnp.zeros((row_count,), jnp.float32),
        jnp.zeros((row_count,), jnp.float32)[:, None] + jnp.zeros((1, latent_width), jnp.float32),
    )


def project_out(final_state, token_count, head_count, latent_width, value_up, output_weight):
    running_max, running_sum, summed = final_state
    mixed_latent = (
        (summed / running_sum[:, None])
        .astype(jnp.bfloat16)
        .reshape(token_count, head_count, latent_width)
    )
    head_out = jnp.einsum(
        "thl,hlv->thv", mixed_latent, value_up, preferred_element_type=jnp.float32
    ).astype(jnp.bfloat16)
    head_out = head_out.reshape(token_count, head_count * value_up.shape[2])
    return jnp.dot(head_out, output_weight, preferred_element_type=jnp.float32)


def on_device(query_plain, query_rotary, latent_keys, span_order, key_up, value_up, output_weight):
    local_tokens = query_plain.shape[0]
    head_count = key_up.shape[0]
    plain_width = key_up.shape[1]
    latent_width = key_up.shape[2]
    rotary_width = query_rotary.shape[1] // head_count
    span_len = local_tokens // 2
    score_scale = 1.0 / math.sqrt(plain_width + rotary_width)
    first_row = lax.axis_index("ctx") * local_tokens
    query_places = token_places(
        span_order, first_row + jnp.arange(local_tokens, dtype=jnp.int32), span_len
    )
    absorbed = jnp.einsum(
        "thn,hnl->thl",
        query_plain.reshape(local_tokens, head_count, plain_width),
        key_up,
        preferred_element_type=jnp.float32,
    ).astype(jnp.bfloat16)
    turned = rotate_pairs(
        query_rotary.reshape(local_tokens, head_count, rotary_width).astype(jnp.float32),
        query_places,
    ).astype(jnp.bfloat16)
    queries = jnp.concatenate([absorbed, turned], axis=2).reshape(
        local_tokens * head_count, latent_width + rotary_width
    )
    row_places = jnp.repeat(query_places, head_count)
    own_rows = latent_keys.shape[0]
    own_first = first_row + lax.axis_index("tp") * own_rows
    own_places = token_places(
        span_order, own_first + jnp.arange(own_rows, dtype=jnp.int32), span_len
    )
    own_turned = rotate_pairs(latent_keys[:, latent_width:].astype(jnp.float32), own_places).astype(
        jnp.bfloat16
    )
    own_keys = jnp.concatenate([latent_keys[:, :latent_width], own_turned], axis=1)
    latest = jnp.max(query_places)
    folder = make_folder(
        queries, row_places, latest, span_order, span_len, latent_width, score_scale
    )
    group_keys = lax.all_gather(own_keys, "tp", axis=0, tiled=True)
    final_state = folder(
        start_state(local_tokens * head_count, latent_width),
        lax.all_gather(group_keys, "ctx", axis=0, tiled=True),
        jnp.int32(0),
    )
    head_terms = project_out(
        final_state, local_tokens, head_count, latent_width, value_up, output_weight
    )
    return lax.psum_scatter(head_terms.astype(jnp.bfloat16), "tp", scatter_dimension=1, tiled=True)


MESH = pl.DeviceIdType.MESH


def split_axes(mesh):
    ctx, tp = mesh.shape["ctx"], mesh.shape["tp"]
    x_size = 1
    while (2 * x_size) ** 2 <= ctx and ctx % (2 * x_size) == 0:
        x_size *= 2
    return ctx // x_size, x_size, tp // 2, 2


def fused_kernel(dims, span_len, latent, span_ref, own_ref, qp_hbm, qr_hbm, ku_hbm, vu_hbm, w_hbm,
                 out_ref, qp, qr, ku, vu, w, keys, queries, scores, heads_out,
                 own_part, sib_out, sib_in, y_out, y_in,
                 load_sem, zs, zr, xs, xr, ys, yr, ss, sr, rss, rsr, rys, ryr):
    Z, X, Y, C = dims
    TP = Y * C
    ctx = lax.axis_index("ctx")
    tp = lax.axis_index("tp")
    z, x = ctx // X, ctx % X
    y, c = tp // C, tp % C
    R = own_ref.shape[0]
    rope = own_ref.shape[1] - latent
    T = qp.shape[0]
    H, plain = ku.shape[0], ku.shape[1]
    L = C * Z * R
    cols = out_ref.shape[1]
    scale = math.log2(math.e) / math.sqrt(plain + rope)

    loads = []
    for n, (src, dst) in enumerate(((qr_hbm, qr), (qp_hbm, qp), (ku_hbm, ku), (vu_hbm, vu), (w_hbm, w))):
        load = pltpu.make_async_copy(src, dst, load_sem.at[n])
        load.start()
        loads.append(load)

    def z_dev(k):
        return (lax.rem(z + k, Z) * X + x, tp)

    def a_dev(k):
        return (z * X + lax.rem(x + k * (1 - c), X), lax.rem(y + k * c, Y) * C + c)

    def b_dev(k):
        return (z * X + lax.rem(x + k * c, X), lax.rem(y + k * (1 - c), Y) * C + c)

    def y_dev(k):
        return (ctx, lax.rem(y + k, Y) * C + c)

    sibling = (ctx, y * C + (C - 1 - c))

    barrier = pltpu.get_barrier_semaphore()
    peers = [z_dev(k) for k in range(1, Z)] + [a_dev(k) for k in range(1, X)]
    peers += [b_dev(k) for k in range(1, Y)] + [sibling]
    for peer in peers:
        pl.semaphore_signal(barrier, inc=1, device_id=peer, device_id_type=MESH)

    lane = lax.broadcasted_iota(jnp.int32, (1, 128), 1)
    pair = lax.rem(lane, rope // 2)
    frequency = jnp.zeros((1, 128), jnp.float32)
    for i in range(rope // 2):
        frequency = jnp.where(pair == i, rope_base ** (-2.0 * i / rope), frequency)
    low = lax.rem(lane, rope) < rope // 2

    def tables(places):
        angles = places.astype(jnp.float32) * frequency
        sine = jnp.sin(angles)
        return jnp.cos(angles), jnp.where(low, -sine, sine)

    def rotate(values, cosine, sine):
        swapped = jnp.where(
            low, pltpu.roll(values, 128 - rope // 2, 1), pltpu.roll(values, rope // 2, 1)
        )
        return values * cosine + swapped * sine

    def place_of(row):
        return span_ref[row // span_len] * span_len + lax.rem(row, span_len)

    own_row = ctx * T + tp * R
    own_places = place_of(own_row) + lax.broadcasted_iota(jnp.int32, (R, 1), 0)
    part = own_ref[:, latent:].astype(jnp.float32)
    turned = rotate(jnp.concatenate([part, part], axis=1), *tables(own_places)).astype(jnp.bfloat16)

    def block(xx, yy, cc, zz):
        return (((xx * Y + yy) * C + cc) * Z + zz) * R

    def rows_at(start, size):
        return keys.at[pl.ds(pl.multiple_of(start, R), size)]

    mine = pl.ds(pl.multiple_of(block(x, y, c, z), R), R)
    keys[mine, :latent] = own_ref[:, :latent]
    keys[mine, latent:] = turned

    pl.semaphore_wait(barrier, len(peers))

    def back(value, k, size):
        return lax.rem(value - k + size, size)

    sends = []

    def send(ref, send_sem, recv_sem, device):
        copy = pltpu.make_async_remote_copy(ref, ref, send_sem, recv_sem, device, MESH)
        copy.start()
        sends.append(copy)

    def await_block(ref, send_sem, recv_sem, device):
        pltpu.make_async_remote_copy(ref, ref, send_sem, recv_sem, device, MESH).wait_recv()

    def line_of(m, j):
        return back(x, m * (1 - c) + j * c, X), back(y, m * c + j * (1 - c), Y)

    def send_a(n):
        ref = rows_at(block(x, y, c, back(z, n, Z)), R)
        for j in range(1, X):
            send(ref, xs.at[j - 1, n], xr.at[j - 1, n], a_dev(j))

    def send_b(m, n):
        ref = rows_at(block(*line_of(m, 0), c, back(z, n, Z)), R)
        for j in range(1, Y):
            send(ref, ys.at[j - 1, m * Z + n], yr.at[j - 1, m * Z + n], b_dev(j))

    for k in range(1, Z):
        send(rows_at(block(x, y, c, z), R), zs.at[k - 1], zr.at[k - 1], z_dev(k))
    send_a(0)
    send_b(0, 0)

    token = lax.broadcasted_iota(jnp.int32, (T, 1), 0)
    query_places = jnp.zeros((T, 1), jnp.int32)
    for n in range(T // span_len):
        query_places = jnp.where(
            token // span_len == n, place_of(ctx * T + n * span_len) + lax.rem(token, span_len), query_places
        )
    cosine, sine = tables(query_places)
    first = lane < rope
    loads[0].wait()

    def turn(n, carry):
        values = qr[:, pl.ds(pl.multiple_of(n * 128, 128), 128)].astype(jnp.float32)
        value = rotate(values, cosine, sine)
        row = pl.multiple_of(2 * n * T, T)
        queries[pl.ds(row, T), latent:] = jnp.where(first, value, 0.0).astype(jnp.bfloat16)
        queries[pl.ds(row + T, T), latent:] = jnp.where(first, 0.0, value).astype(jnp.bfloat16)
        return carry

    lax.fori_loop(0, H // 2, turn, 0)
    loads[1].wait()
    loads[2].wait()

    def absorb(n, carry):
        value = jnp.dot(
            qp[:, pl.ds(pl.multiple_of(n * plain, plain), plain)], ku[n], preferred_element_type=jnp.float32
        )
        queries[pl.ds(pl.multiple_of(n * T, T), T), :latent] = value.astype(jnp.bfloat16)
        return carry

    lax.fori_loop(0, H, absorb, 0)

    group = 8
    key_lane = lax.broadcasted_iota(jnp.int32, (1, L), 1)

    def score_line(xx, yy):
        key_places = jnp.zeros((1, L), jnp.int32)
        for b in range(C * Z):
            start = ((b % Z * X + xx) * TP + yy * C + b // Z) * R
            key_places = jnp.where(key_lane // R == b, place_of(start) + lax.rem(key_lane, R), key_places)
        allowed = key_places <= query_places
        line = xx * Y + yy
        line_keys = rows_at(block(xx, yy, 0, 0), L)

        def step(n, carry):
            start = pl.multiple_of(n * (group * T), group * T)
            value = lax.dot_general(
                queries[pl.ds(start, group * T), :], line_keys[...],
                (((1,), (1,)), ((), ())), preferred_element_type=jnp.float32,
            ) * scale
            for g in range(group):
                scores[line, pl.ds(start + g * T, T), :] = jnp.where(
                    allowed, value[g * T:(g + 1) * T], fill_score
                )
            return carry

        lax.fori_loop(0, H // group, step, 0)

    def sib_refs(m, j, cc):
        return rows_at(block(*line_of(m, j), cc, 0), Z * R)

    def receive_line(m, j):
        for n in range(Z):
            ref = rows_at(block(*line_of(m, j), c, back(z, n, Z)), R)
            if j > 0:
                await_block(ref, ys.at[j - 1, m * Z + n], yr.at[j - 1, m * Z + n], b_dev(j))
            elif m > 0:
                await_block(ref, xs.at[m - 1, n], xr.at[m - 1, n], a_dev(m))
                send_b(m, n)
            elif n > 0:
                await_block(ref, zs.at[n - 1], zr.at[n - 1], z_dev(n))
                send_a(n)
                send_b(0, n)
        send(sib_refs(m, j, c), ss.at[j * X + m], sr.at[j * X + m], sibling)

    def finish_line(m, j):
        n = m * X + j
        await_block(sib_refs(m, j, C - 1 - c), ss.at[n], sr.at[n], sibling)
        score_line(*line_of(m, j))

    stages = [(m, 0) for m in range(X)] + [(m, j) for j in range(1, Y) for m in range(X)]
    done = []
    for index, line in enumerate(stages):
        receive_line(*line)
        passed = stages[:index]
        for m, j in passed:
            if (m, j) not in done and (j, m) in passed:
                finish_line(m, j)
                done.append((m, j))
    for line in stages:
        if line not in done:
            finish_line(*line)

    loads[3].wait()

    def attend(n, carry):
        start = pl.multiple_of(n * T, T)
        parts = [scores[l, pl.ds(start, T), :] for l in range(X * Y)]
        highest = parts[0]
        for part in parts[1:]:
            highest = jnp.maximum(highest, part)
        highest = jnp.max(highest, axis=1, keepdims=True)
        total = jnp.zeros((T, L), jnp.float32)
        weights = []
        for part in parts:
            raised = jnp.exp2(part - highest)
            total = total + raised
            weights.append(raised.astype(jnp.bfloat16))
        summed = jnp.dot(
            jnp.concatenate(weights, axis=1), keys[:, :latent], preferred_element_type=jnp.float32
        )
        context = (summed * (1.0 / jnp.sum(total, axis=1, keepdims=True))).astype(jnp.bfloat16)
        value = jnp.dot(context, vu[n], preferred_element_type=jnp.float32).astype(jnp.bfloat16)
        width = vu.shape[2]
        heads_out[:, pl.ds(pl.multiple_of(n * width, width), width)] = value
        return carry

    lax.fori_loop(0, H, attend, 0, unroll=4)
    loads[4].wait()

    def project(owner):
        return jnp.dot(
            heads_out[...], w[:, pl.ds(pl.multiple_of(owner * cols, 128), cols)],
            preferred_element_type=jnp.float32,
        )

    for j in range(Y - 1, -1, -1):
        target = lax.rem(y + j, Y) * C
        sib_out[j] = project(target + C - 1 - c).astype(jnp.bfloat16)
        copy = pltpu.make_async_remote_copy(sib_out.at[j], sib_in.at[j], rss.at[j], rsr.at[j], sibling, MESH)
        copy.start()
        own_part[...] = project(target + c)
        copy.wait_recv()
        sends.append(copy)
        if j > 0:
            y_out[j - 1] = (own_part[...] + sib_in[j].astype(jnp.float32)).astype(jnp.bfloat16)
            copy = pltpu.make_async_remote_copy(
                y_out.at[j - 1], y_in.at[j - 1], rys.at[j - 1], ryr.at[j - 1], y_dev(j), MESH
            )
            copy.start()
            sends.append(copy)
    result = own_part[...] + sib_in[0].astype(jnp.float32)
    for j in range(1, Y):
        pltpu.make_async_remote_copy(
            y_out.at[j - 1], y_in.at[j - 1], rys.at[j - 1], ryr.at[j - 1], y_dev(j), MESH
        ).wait_recv()
        result = result + y_in[j - 1].astype(jnp.float32)
    out_ref[...] = result.astype(out_ref.dtype)
    for copy in sends:
        copy.wait_send()


def fused(dims, query_plain, query_rotary, latent_keys, span_order, key_up, value_up, output_weight):
    Z, X, Y, C = dims
    T = query_plain.shape[0]
    R = latent_keys.shape[0]
    H, plain, latent = key_up.shape
    tokens = R * Z * X * Y * C
    span_len = tokens // span_order.shape[0]
    cols = output_weight.shape[1] // (Y * C)
    bf16 = jnp.bfloat16
    dma = pltpu.SemaphoreType.DMA
    any_space = pl.BlockSpec(memory_space=pl.ANY)
    return pl.pallas_call(
        partial(fused_kernel, dims, span_len, latent),
        out_shape=jax.ShapeDtypeStruct((T, cols), bf16),
        in_specs=[
            pl.BlockSpec(memory_space=pltpu.SMEM),
            pl.BlockSpec(memory_space=pltpu.VMEM),
        ] + [any_space] * 5,
        out_specs=pl.BlockSpec(memory_space=pltpu.VMEM),
        scratch_shapes=[
            pltpu.VMEM(query_plain.shape, bf16),
            pltpu.VMEM(query_rotary.shape, bf16),
            pltpu.VMEM(key_up.shape, bf16),
            pltpu.VMEM(value_up.shape, bf16),
            pltpu.VMEM(output_weight.shape, bf16),
            pltpu.VMEM((tokens, latent + 128), bf16),
            pltpu.VMEM((H * T, latent + 128), bf16),
            pltpu.VMEM((X * Y, H * T, C * Z * R), jnp.float32),
            pltpu.VMEM((T, H * value_up.shape[2]), bf16),
            pltpu.VMEM((T, cols), jnp.float32),
            pltpu.VMEM((Y, T, cols), bf16),
            pltpu.VMEM((Y, T, cols), bf16),
            pltpu.VMEM((Y - 1, T, cols), bf16),
            pltpu.VMEM((Y - 1, T, cols), bf16),
            dma((5,)),
            dma((Z - 1,)), dma((Z - 1,)),
            dma((X - 1, Z)), dma((X - 1, Z)),
            dma((Y - 1, X * Z)), dma((Y - 1, X * Z)),
            dma((X * Y,)), dma((X * Y,)),
            dma((Y,)), dma((Y,)),
            dma((Y - 1,)), dma((Y - 1,)),
        ],
        compiler_params=pltpu.CompilerParams(
            collective_id=0, has_side_effects=True, vmem_limit_bytes=56 * 1024 * 1024
        ),
    )(span_order, latent_keys, query_plain, query_rotary, key_up, value_up, output_weight)


def chosen(mesh, *arrays):
    dims = split_axes(mesh)
    Z, X, Y, C = dims
    query_plain, query_rotary, latent_keys, span_order, key_up, value_up, output_weight = arrays
    R, T = latent_keys.shape[0], query_plain.shape[0]
    rope = latent_keys.shape[1] - key_up.shape[2]
    cols = output_weight.shape[1] // mesh.shape["tp"]
    fits = min(Z, X, Y) > 1 and X == Y and mesh.shape["tp"] % 2 == 0 and R % 16 == 0 and cols % 128 == 0
    fits = fits and rope * 2 == 128 and (C * Z * R) % 128 == 0 and key_up.shape[0] % 8 == 0
    return fused(dims, *arrays) if fits else on_device(*arrays)


def solution(mesh):
    return jax.shard_map(
        partial(chosen, mesh),
        mesh=mesh,
        in_specs=(
            P("ctx", "tp"),
            P("ctx", "tp"),
            P(("ctx", "tp"), None),
            P(),
            P("tp", None, None),
            P("tp", None, None),
            P("tp", None),
        ),
        out_specs=P("ctx", "tp"),
        check_vma=False,
    )
```

profile of v0, /device:TPU:0, one launch (start us, length us, event | category | flops | bytes accessed | tf_op | source)
XLA Modules:
  0.0 39.1 jit_solution(12500974124873759276)
XLA Ops:
  0.0 37.4 %shard_map.73 = bf16[128,896]{1,0:T(8,128)(2,1)} custom-call(s32[16]{0:T(128)} %span_ref.1, bf16[32,576]{1,0:T(8,128)(2,1)} %own_ref.1, bf16[128,2048]{1,0:T(8,128)(2,1)} %qp_hbm.1, bf16[128,1024]{1,0:T(8,128)(2,1)} %qr_hbm.1, bf16[16,128,512]{2,1,0:T(8,128)(2,1)} %ku_hbm.1, bf16[16,512,128]{2,1,0:T(8,128)(2,1)} %vu_hbm.1, bf16[2048,3584]{1,0:T(8,128)(2,1)} %w_hbm.1), custom_call_target="tpu_custom_call" | custom-call | tf_op jit(solution)/shard_map/pallas_call | solution.py:467
  37.4 1.6 %copy.9 = bf16[128,896]{1,0:T(8,128)(2,1)} copy(bf16[128,896]{1,0:T(8,128)(2,1)} %shard_map.73) | data formatting | bytes 458752
where the time goes:
time: 39.3 us; the launch traced here: 39.1 us
  Pallas kernels  37.4 us (95%)
  local copies, waits for them, and re-layouts  1.65 us (4%)
    pallas_call x1, Pallas kernels, fused(): pl.pallas_call(partial(fused_kernel, dims, span_len, latent), out_shape=j...  37.4 us
    unnamed x1, local copies, waits for them, and re-layouts  1.65 us

commit v1 on v0

--- a/solution.py
+++ b/solution.py
@@ -189,12 +189,11 @@
     return ctx // x_size, x_size, tp // 2, 2
 
 
-def fused_kernel(dims, span_len, latent, span_ref, own_ref, qp_hbm, qr_hbm, ku_hbm, vu_hbm, w_hbm,
-                 out_ref, qp, qr, ku, vu, w, keys, queries, scores, heads_out,
-                 own_part, sib_out, sib_in, y_out, y_in,
-                 load_sem, zs, zr, xs, xr, ys, yr, ss, sr, rss, rsr, rys, ryr):
+def fused_kernel(dims, span_len, latent, span_hbm, own_hbm, qp_hbm, qr_hbm, ku_hbm, vu_hbm, w_hbm,
+                 out_ref, span_ref, own_ref, qp, qr, ku, vu, w, keys, queries, bias, scores, acc, top, total,
+                 heads_out, own_part, sib_out, sib_in, y_out, y_in,
+                 load_sem, zs, zr, ps, pr, ss, sr, rss, rsr, rys, ryr):
     Z, X, Y, C = dims
-    TP = Y * C
     ctx = lax.axis_index("ctx")
     tp = lax.axis_index("tp")
     z, x = ctx // X, ctx % X
@@ -203,35 +202,38 @@
     rope = own_ref.shape[1] - latent
     T = qp.shape[0]
     H, plain = ku.shape[0], ku.shape[1]
-    L = C * Z * R
+    L = X * Y * C * R
     cols = out_ref.shape[1]
     scale = math.log2(math.e) / math.sqrt(plain + rope)
 
+    def z_dev(zz):
+        return (zz * X + x, tp)
+
+    sibling = (ctx, y * C + (C - 1 - c))
+    y_peer = (ctx, (1 - y) * C + c)
+    plane_devs = [(z * X + 1 - x, tp), y_peer, (z * X + 1 - x, (1 - y) * C + c)]
+
+    def plane_cols(kind):
+        return [(x, y), (1 - x, y), (x, 1 - y), (1 - x, 1 - y)][kind]
+
+    def z_order(i):
+        low = i + (i >= z).astype(jnp.int32)
+        high = Z - 1 - i - (i >= Z - 1 - z).astype(jnp.int32)
+        return jnp.where(z < Z // 2, low, high)
+
+    planes = [z] + [z_order(jnp.int32(i)) for i in range(Z - 1)]
+
+    barrier = pltpu.get_barrier_semaphore()
+    peers = [z_dev(zz) for zz in planes[1:]] + plane_devs + [sibling]
+    for peer in peers:
+        pl.semaphore_signal(barrier, inc=1, device_id=peer, device_id_type=MESH)
+
     loads = []
-    for n, (src, dst) in enumerate(((qr_hbm, qr), (qp_hbm, qp), (ku_hbm, ku), (vu_hbm, vu), (w_hbm, w))):
+    pairs = ((own_hbm, own_ref), (span_hbm, span_ref), (qr_hbm, qr), (qp_hbm, qp), (ku_hbm, ku), (vu_hbm, vu), (w_hbm, w))
+    for n, (src, dst) in enumerate(pairs):
         load = pltpu.make_async_copy(src, dst, load_sem.at[n])
         load.start()
         loads.append(load)
-
-    def z_dev(k):
-        return (lax.rem(z + k, Z) * X + x, tp)
-
-    def a_dev(k):
-        return (z * X + lax.rem(x + k * (1 - c), X), lax.rem(y + k * c, Y) * C + c)
-
-    def b_dev(k):
-        return (z * X + lax.rem(x + k * c, X), lax.rem(y + k * (1 - c), Y) * C + c)
-
-    def y_dev(k):
-        return (ctx, lax.rem(y + k, Y) * C + c)
-
-    sibling = (ctx, y * C + (C - 1 - c))
-
-    barrier = pltpu.get_barrier_semaphore()
-    peers = [z_dev(k) for k in range(1, Z)] + [a_dev(k) for k in range(1, X)]
-    peers += [b_dev(k) for k in range(1, Y)] + [sibling]
-    for peer in peers:
-        pl.semaphore_signal(barrier, inc=1, device_id=peer, device_id_type=MESH)
 
     lane = lax.broadcasted_iota(jnp.int32, (1, 128), 1)
     pair = lax.rem(lane, rope // 2)
@@ -254,53 +256,22 @@
     def place_of(row):
         return span_ref[row // span_len] * span_len + lax.rem(row, span_len)
 
+    loads[0].wait()
+    loads[1].wait()
     own_row = ctx * T + tp * R
     own_places = place_of(own_row) + lax.broadcasted_iota(jnp.int32, (R, 1), 0)
     part = own_ref[:, latent:].astype(jnp.float32)
     turned = rotate(jnp.concatenate([part, part], axis=1), *tables(own_places)).astype(jnp.bfloat16)
 
-    def block(xx, yy, cc, zz):
-        return (((xx * Y + yy) * C + cc) * Z + zz) * R
+    def block(zz, xx, yy, cc):
+        return (((zz * X + xx) * Y + yy) * C + cc) * R
 
     def rows_at(start, size):
         return keys.at[pl.ds(pl.multiple_of(start, R), size)]
 
-    mine = pl.ds(pl.multiple_of(block(x, y, c, z), R), R)
+    mine = pl.ds(pl.multiple_of(own_row, R), R)
     keys[mine, :latent] = own_ref[:, :latent]
     keys[mine, latent:] = turned
-
-    pl.semaphore_wait(barrier, len(peers))
-
-    def back(value, k, size):
-        return lax.rem(value - k + size, size)
-
-    sends = []
-
-    def send(ref, send_sem, recv_sem, device):
-        copy = pltpu.make_async_remote_copy(ref, ref, send_sem, recv_sem, device, MESH)
-        copy.start()
-        sends.append(copy)
-
-    def await_block(ref, send_sem, recv_sem, device):
-        pltpu.make_async_remote_copy(ref, ref, send_sem, recv_sem, device, MESH).wait_recv()
-
-    def line_of(m, j):
-        return back(x, m * (1 - c) + j * c, X), back(y, m * c + j * (1 - c), Y)
-
-    def send_a(n):
-        ref = rows_at(block(x, y, c, back(z, n, Z)), R)
-        for j in range(1, X):
-            send(ref, xs.at[j - 1, n], xr.at[j - 1, n], a_dev(j))
-
-    def send_b(m, n):
-        ref = rows_at(block(*line_of(m, 0), c, back(z, n, Z)), R)
-        for j in range(1, Y):
-            send(ref, ys.at[j - 1, m * Z + n], yr.at[j - 1, m * Z + n], b_dev(j))
-
-    for k in range(1, Z):
-        send(rows_at(block(x, y, c, z), R), zs.at[k - 1], zr.at[k - 1], z_dev(k))
-    send_a(0)
-    send_b(0, 0)
 
     token = lax.broadcasted_iota(jnp.int32, (T, 1), 0)
     query_places = jnp.zeros((T, 1), jnp.int32)
@@ -310,116 +281,155 @@
         )
     cosine, sine = tables(query_places)
     first = lane < rope
-    loads[0].wait()
+    loads[2].wait()
 
     def turn(n, carry):
         values = qr[:, pl.ds(pl.multiple_of(n * 128, 128), 128)].astype(jnp.float32)
-        value = rotate(values, cosine, sine)
+        value = rotate(values, cosine, sine) * scale
         row = pl.multiple_of(2 * n * T, T)
         queries[pl.ds(row, T), latent:] = jnp.where(first, value, 0.0).astype(jnp.bfloat16)
         queries[pl.ds(row + T, T), latent:] = jnp.where(first, 0.0, value).astype(jnp.bfloat16)
         return carry
 
     lax.fori_loop(0, H // 2, turn, 0)
-    loads[1].wait()
-    loads[2].wait()
+    key_lane = lax.broadcasted_iota(jnp.int32, (1, L), 1)
+    for n, plane in enumerate(planes):
+        key_places = jnp.zeros((1, L), jnp.int32)
+        for b in range(L // span_len):
+            start = plane * L + b * span_len
+            key_places = jnp.where(key_lane // span_len == b, place_of(start) + lax.rem(key_lane, span_len), key_places)
+        bias[n] = jnp.where(key_places <= query_places, 0.0, fill_score)
+    loads[3].wait()
+    loads[4].wait()
 
     def absorb(n, carry):
         value = jnp.dot(
             qp[:, pl.ds(pl.multiple_of(n * plain, plain), plain)], ku[n], preferred_element_type=jnp.float32
         )
-        queries[pl.ds(pl.multiple_of(n * T, T), T), :latent] = value.astype(jnp.bfloat16)
+        queries[pl.ds(pl.multiple_of(n * T, T), T), :latent] = (value * scale).astype(jnp.bfloat16)
         return carry
 
-    lax.fori_loop(0, H, absorb, 0)
+    lax.fori_loop(0, H, absorb, 0, unroll=4)
+
+    pl.semaphore_wait(barrier, len(peers))
+    sends = []
+
+    def send(ref, send_sem, recv_sem, device):
+        copy = pltpu.make_async_remote_copy(ref, ref, send_sem, recv_sem, device, MESH)
+        copy.start()
+        sends.append(copy)
+
+    def arrival(ref, send_sem, recv_sem, device):
+        pltpu.make_async_remote_copy(ref, ref, send_sem, recv_sem, device, MESH).wait_recv()
+
+    def send_sibling(n, kind):
+        ref = rows_at(block(planes[n], *plane_cols(kind), c), R)
+        send(ref, ss.at[n, kind], sr.at[n, kind], sibling)
+
+    def send_plane(n):
+        ref = rows_at(block(planes[n], x, y, c), R)
+        for kind in (2, 0, 1):
+            send(ref, ps.at[kind, n], pr.at[kind, planes[n]], plane_devs[kind])
+        send_sibling(n, 0)
+
+    def relay_plane(n):
+        zz = planes[n]
+        arrival(rows_at(block(zz, x, y, c), R), zs.at[n - 1], zr.at[zz], z_dev(zz))
+        send_plane(n)
+
+    def relay_sibling(n):
+        for kind in (0, 1, 2):
+            ref = rows_at(block(planes[n], *plane_cols(kind + 1), c), R)
+            arrival(ref, ps.at[kind, n], pr.at[kind, planes[n]], plane_devs[kind])
+            send_sibling(n, kind + 1)
+
+    def await_sibling(n):
+        for kind in range(4):
+            ref = rows_at(block(planes[n], *plane_cols(kind), C - 1 - c), R)
+            arrival(ref, ss.at[n, kind], sr.at[n, kind], sibling)
 
     group = 8
-    key_lane = lax.broadcasted_iota(jnp.int32, (1, L), 1)
-
-    def score_line(xx, yy):
-        key_places = jnp.zeros((1, L), jnp.int32)
-        for b in range(C * Z):
-            start = ((b % Z * X + xx) * TP + yy * C + b // Z) * R
-            key_places = jnp.where(key_lane // R == b, place_of(start) + lax.rem(key_lane, R), key_places)
-        allowed = key_places <= query_places
-        line = xx * Y + yy
-        line_keys = rows_at(block(xx, yy, 0, 0), L)
-
-        def step(n, carry):
-            start = pl.multiple_of(n * (group * T), group * T)
+
+    def plane_rows(n):
+        return pl.ds(pl.multiple_of(planes[n] * L, L), L)
+
+    def score(n):
+        def step(m, carry):
+            start = pl.multiple_of(m * (group * T), group * T)
             value = lax.dot_general(
-                queries[pl.ds(start, group * T), :], line_keys[...],
+                queries[pl.ds(start, group * T), :], keys[plane_rows(n), :],
                 (((1,), (1,)), ((), ())), preferred_element_type=jnp.float32,
-            ) * scale
+            )
             for g in range(group):
-                scores[line, pl.ds(start + g * T, T), :] = jnp.where(
-                    allowed, value[g * T:(g + 1) * T], fill_score
+                scores[n, pl.ds(start + g * T, T), :] = value[g * T:(g + 1) * T] + bias[n]
+            return carry
+
+        lax.fori_loop(0, H // group, step, 0)
+
+    def attend(members, opening, closing):
+        def step(h, carry):
+            rows = pl.ds(pl.multiple_of(h * T, T), T)
+            tiles = [scores[n, rows, k:k + 128] for n in members for k in range(0, L, 128)]
+            highest = tiles[0]
+            for tile in tiles[1:]:
+                highest = jnp.maximum(highest, tile)
+            highest = jnp.max(highest, axis=1, keepdims=True)
+            if not opening:
+                before = top[rows, :1]
+                highest = jnp.maximum(highest, before)
+                factor = jnp.exp2(before - highest)
+            weights = []
+            sums = None
+            for tile in tiles:
+                raised = jnp.exp2(tile - highest)
+                sums = raised if sums is None else sums + raised
+                weights.append(raised.astype(jnp.bfloat16))
+            summed = None
+            per = L // 128
+            for i, n in enumerate(members):
+                value = jnp.dot(
+                    jnp.concatenate(weights[i * per:(i + 1) * per], axis=1), keys[plane_rows(n), :latent],
+                    preferred_element_type=jnp.float32,
                 )
+                summed = value if summed is None else summed + value
+            if not opening:
+                sums = sums + total[rows, :] * factor
+                summed = summed + acc[rows, :] * factor
+            if closing:
+                context = (summed * (1.0 / jnp.sum(sums, axis=1, keepdims=True))).astype(jnp.bfloat16)
+                value = jnp.dot(context, vu[h], preferred_element_type=jnp.float32).astype(jnp.bfloat16)
+                width = vu.shape[2]
+                heads_out[:, pl.ds(pl.multiple_of(h * width, width), width)] = value
+            else:
+                top[rows, :] = jnp.broadcast_to(highest, (T, 128))
+                total[rows, :] = sums
+                acc[rows, :] = summed
             return carry
 
-        lax.fori_loop(0, H // group, step, 0)
-
-    def sib_refs(m, j, cc):
-        return rows_at(block(*line_of(m, j), cc, 0), Z * R)
-
-    def receive_line(m, j):
-        for n in range(Z):
-            ref = rows_at(block(*line_of(m, j), c, back(z, n, Z)), R)
-            if j > 0:
-                await_block(ref, ys.at[j - 1, m * Z + n], yr.at[j - 1, m * Z + n], b_dev(j))
-            elif m > 0:
-                await_block(ref, xs.at[m - 1, n], xr.at[m - 1, n], a_dev(m))
-                send_b(m, n)
-            elif n > 0:
-                await_block(ref, zs.at[n - 1], zr.at[n - 1], z_dev(n))
-                send_a(n)
-                send_b(0, n)
-        send(sib_refs(m, j, c), ss.at[j * X + m], sr.at[j * X + m], sibling)
-
-    def finish_line(m, j):
-        n = m * X + j
-        await_block(sib_refs(m, j, C - 1 - c), ss.at[n], sr.at[n], sibling)
-        score_line(*line_of(m, j))
-
-    stages = [(m, 0) for m in range(X)] + [(m, j) for j in range(1, Y) for m in range(X)]
-    done = []
-    for index, line in enumerate(stages):
-        receive_line(*line)
-        passed = stages[:index]
-        for m, j in passed:
-            if (m, j) not in done and (j, m) in passed:
-                finish_line(m, j)
-                done.append((m, j))
-    for line in stages:
-        if line not in done:
-            finish_line(*line)
-
-    loads[3].wait()
-
-    def attend(n, carry):
-        start = pl.multiple_of(n * T, T)
-        parts = [scores[l, pl.ds(start, T), :] for l in range(X * Y)]
-        highest = parts[0]
-        for part in parts[1:]:
-            highest = jnp.maximum(highest, part)
-        highest = jnp.max(highest, axis=1, keepdims=True)
-        total = jnp.zeros((T, L), jnp.float32)
-        weights = []
-        for part in parts:
-            raised = jnp.exp2(part - highest)
-            total = total + raised
-            weights.append(raised.astype(jnp.bfloat16))
-        summed = jnp.dot(
-            jnp.concatenate(weights, axis=1), keys[:, :latent], preferred_element_type=jnp.float32
-        )
-        context = (summed * (1.0 / jnp.sum(total, axis=1, keepdims=True))).astype(jnp.bfloat16)
-        value = jnp.dot(context, vu[n], preferred_element_type=jnp.float32).astype(jnp.bfloat16)
-        width = vu.shape[2]
-        heads_out[:, pl.ds(pl.multiple_of(n * width, width), width)] = value
-        return carry
-
-    lax.fori_loop(0, H, attend, 0, unroll=4)
-    loads[4].wait()
+        lax.fori_loop(0, H, step, 0, unroll=4)
+
+    for n in range(1, Z):
+        send(rows_at(own_row, R), zs.at[n - 1], zr.at[z], z_dev(planes[n]))
+    send_plane(0)
+
+    relay_sibling(0)
+    for n in range(1, Z - 1):
+        relay_plane(n)
+    await_sibling(0)
+    score(0)
+    relay_plane(Z - 1)
+    relay_sibling(1)
+    attend([0], True, False)
+    for n in range(1, Z):
+        if n + 1 < Z:
+            relay_sibling(n + 1)
+        await_sibling(n)
+        score(n)
+        if n == 1:
+            attend([1], False, False)
+    loads[5].wait()
+    attend(list(range(2, Z)), False, True)
+    loads[6].wait()
 
     def project(owner):
         return jnp.dot(
@@ -427,7 +437,7 @@
             preferred_element_type=jnp.float32,
         )
 
-    for j in range(Y - 1, -1, -1):
+    for j in (1, 0):
         target = lax.rem(y + j, Y) * C
         sib_out[j] = project(target + C - 1 - c).astype(jnp.bfloat16)
         copy = pltpu.make_async_remote_copy(sib_out.at[j], sib_in.at[j], rss.at[j], rsr.at[j], sibling, MESH)
@@ -436,43 +446,38 @@
         copy.wait_recv()
         sends.append(copy)
         if j > 0:
-            y_out[j - 1] = (own_part[...] + sib_in[j].astype(jnp.float32)).astype(jnp.bfloat16)
-            copy = pltpu.make_async_remote_copy(
-                y_out.at[j - 1], y_in.at[j - 1], rys.at[j - 1], ryr.at[j - 1], y_dev(j), MESH
-            )
-            copy.start()
-            sends.append(copy)
+            y_out[...] = (own_part[...] + sib_in[j].astype(jnp.float32)).astype(jnp.bfloat16)
+            y_copy = pltpu.make_async_remote_copy(y_out, y_in, rys.at[0], ryr.at[0], y_peer, MESH)
+            y_copy.start()
+            sends.append(y_copy)
     result = own_part[...] + sib_in[0].astype(jnp.float32)
-    for j in range(1, Y):
-        pltpu.make_async_remote_copy(
-            y_out.at[j - 1], y_in.at[j - 1], rys.at[j - 1], ryr.at[j - 1], y_dev(j), MESH
-        ).wait_recv()
-        result = result + y_in[j - 1].astype(jnp.float32)
-    out_ref[...] = result.astype(out_ref.dtype)
+    y_copy.wait_recv()
+    out_ref[...] = (result + y_in[...].astype(jnp.float32)).astype(out_ref.dtype)
     for copy in sends:
         copy.wait_send()
 
 
-def fused(dims, query_plain, query_rotary, latent_keys, span_order, key_up, value_up, output_weight):
+def fused(dims, *arrays):
     Z, X, Y, C = dims
+    query_plain, query_rotary, latent_keys, span_order, key_up, value_up, output_weight = arrays
     T = query_plain.shape[0]
     R = latent_keys.shape[0]
     H, plain, latent = key_up.shape
     tokens = R * Z * X * Y * C
+    L = X * Y * C * R
     span_len = tokens // span_order.shape[0]
     cols = output_weight.shape[1] // (Y * C)
-    bf16 = jnp.bfloat16
+    bf16, f32 = jnp.bfloat16, jnp.float32
     dma = pltpu.SemaphoreType.DMA
-    any_space = pl.BlockSpec(memory_space=pl.ANY)
+    operands = (span_order, latent_keys, query_plain, query_rotary, key_up, value_up, output_weight)
     return pl.pallas_call(
         partial(fused_kernel, dims, span_len, latent),
-        out_shape=jax.ShapeDtypeStruct((T, cols), bf16),
-        in_specs=[
-            pl.BlockSpec(memory_space=pltpu.SMEM),
-            pl.BlockSpec(memory_space=pltpu.VMEM),
-        ] + [any_space] * 5,
+        out_shape=pltpu.VMEM((T, cols), bf16),
+        in_specs=[pl.BlockSpec(memory_space=pltpu.HBM)] * len(operands),
         out_specs=pl.BlockSpec(memory_space=pltpu.VMEM),
         scratch_shapes=[
+            pltpu.SMEM(span_order.shape, jnp.int32),
+            pltpu.VMEM(latent_keys.shape, bf16),
             pltpu.VMEM(query_plain.shape, bf16),
             pltpu.VMEM(query_rotary.shape, bf16),
             pltpu.VMEM(key_up.shape, bf16),
@@ -480,25 +485,28 @@
             pltpu.VMEM(output_weight.shape, bf16),
             pltpu.VMEM((tokens, latent + 128), bf16),
             pltpu.VMEM((H * T, latent + 128), bf16),
-            pltpu.VMEM((X * Y, H * T, C * Z * R), jnp.float32),
+            pltpu.VMEM((Z, T, L), f32),
+            pltpu.VMEM((Z, H * T, L), f32),
+            pltpu.VMEM((H * T, latent), f32),
+            pltpu.VMEM((H * T, 128), f32),
+            pltpu.VMEM((H * T, 128), f32),
             pltpu.VMEM((T, H * value_up.shape[2]), bf16),
-            pltpu.VMEM((T, cols), jnp.float32),
+            pltpu.VMEM((T, cols), f32),
             pltpu.VMEM((Y, T, cols), bf16),
             pltpu.VMEM((Y, T, cols), bf16),
-            pltpu.VMEM((Y - 1, T, cols), bf16),
-            pltpu.VMEM((Y - 1, T, cols), bf16),
-            dma((5,)),
-            dma((Z - 1,)), dma((Z - 1,)),
-            dma((X - 1, Z)), dma((X - 1, Z)),
-            dma((Y - 1, X * Z)), dma((Y - 1, X * Z)),
-            dma((X * Y,)), dma((X * Y,)),
+            pltpu.VMEM((T, cols), bf16),
+            pltpu.VMEM((T, cols), bf16),
+            dma((7,)),
+            dma((Z - 1,)), dma((Z,)),
+            dma((3, Z)), dma((3, Z)),
+            dma((Z, 4)), dma((Z, 4)),
             dma((Y,)), dma((Y,)),
-            dma((Y - 1,)), dma((Y - 1,)),
+            dma((1,)), dma((1,)),
         ],
         compiler_params=pltpu.CompilerParams(
             collective_id=0, has_side_effects=True, vmem_limit_bytes=56 * 1024 * 1024
         ),
-    )(span_order, latent_keys, query_plain, query_rotary, key_up, value_up, output_weight)
+    )(*(pltpu.with_memory_space_constraint(value, pltpu.HBM) for value in operands))
 
 
 def chosen(mesh, *arrays):
@@ -508,8 +516,8 @@
     R, T = latent_keys.shape[0], query_plain.shape[0]
     rope = latent_keys.shape[1] - key_up.shape[2]
     cols = output_weight.shape[1] // mesh.shape["tp"]
-    fits = min(Z, X, Y) > 1 and X == Y and mesh.shape["tp"] % 2 == 0 and R % 16 == 0 and cols % 128 == 0
-    fits = fits and rope * 2 == 128 and (C * Z * R) % 128 == 0 and key_up.shape[0] % 8 == 0
+    fits = Z > 1 and X == Y == 2 and mesh.shape["tp"] == 4 and R % 16 == 0 and cols % 128 == 0
+    fits = fits and rope * 2 == 128 and (X * Y * C * R) % 128 == 0 and key_up.shape[0] % 8 == 0
     return fused(dims, *arrays) if fits else on_device(*arrays)
 
 

time: 39.3 us -> 36.9 us (0.939)
  Pallas kernels: 37.4 us -> 36.1 us
  local copies, waits for them, and re-layouts: 1.65 us -> 0.69 us
    pallas_call x1, Pallas kernels: 37.4 us -> 36.1 us  [fused(): pl.pallas_call(partial(fused_kernel, dims, span_len, latent), out_shape=p...]
    unnamed x1, local copies, waits for them, and re-layouts: 1.65 us -> 0.69 us
where the time goes in v1:
time: 36.9 us; the launch traced here: 36.8 us
  Pallas kernels  36.1 us (98%)
  local copies, waits for them, and re-layouts  0.69 us (2%)
    pallas_call x1, Pallas kernels, fused(): pl.pallas_call(partial(fused_kernel, dims, span_len, latent), out_shape=p...  36.1 us

profile of v1, /device:TPU:0, one launch (start us, length us, event | category | flops | bytes accessed | tf_op | source)
XLA Modules:
  0.0 36.8 jit_solution(1407335931997895061)
XLA Ops:
  0.0 36.1 %shard_map.73 = bf16[128,896]{1,0:T(8,128)(2,1)S(1)} custom-call(s32[16]{0:T(128)} %span_hbm.1, bf16[32,576]{1,0:T(8,128)(2,1)} %own_hbm.1, bf16[128,2048]{1,0:T(8,128)(2,1)} %qp_hbm.1, bf16[128,1024]{1,0:T(8,128)(2,1)} %qr_hbm.1, bf16[16,128,512]{2,1,0:T(8,128)(2,1)} %ku_hbm.1, bf16[16,512,128]{2,1,0:T(8,128)(2,1)} %vu_hbm.1, bf16[2048,3584]{1,0:T(8,128)(2,1)} %w_hbm.1), custom_call_target="tpu_custom_call" | custom-call | tf_op jit(solution)/shard_map/pallas_call | solution.py:473
  36.1 0.7 %copy.9 = bf16[128,896]{1,0:T(8,128)(2,1)} copy(bf16[128,896]{1,0:T(8,128)(2,1)S(1)} %shard_map.73) | data formatting | bytes 458752

commit v2 on v1

--- a/solution.py
+++ b/solution.py
@@ -366,7 +366,7 @@
 
         lax.fori_loop(0, H // group, step, 0)
 
-    def attend(members, opening, closing):
+    def attend(members, opening, closing, begin=0, end=H):
         def step(h, carry):
             rows = pl.ds(pl.multiple_of(h * T, T), T)
             tiles = [scores[n, rows, k:k + 128] for n in members for k in range(0, L, 128)]
@@ -406,29 +406,29 @@
                 acc[rows, :] = summed
             return carry
 
-        lax.fori_loop(0, H, step, 0, unroll=4)
+        lax.fori_loop(begin, end, step, 0, unroll=8)
 
     for n in range(1, Z):
         send(rows_at(own_row, R), zs.at[n - 1], zr.at[z], z_dev(planes[n]))
     send_plane(0)
 
     relay_sibling(0)
-    for n in range(1, Z - 1):
+    for n in range(1, Z):
         relay_plane(n)
-    await_sibling(0)
-    score(0)
-    relay_plane(Z - 1)
     relay_sibling(1)
-    attend([0], True, False)
-    for n in range(1, Z):
-        if n + 1 < Z:
-            relay_sibling(n + 1)
+    half = Z // 2
+    for n in range(half):
         await_sibling(n)
         score(n)
-        if n == 1:
-            attend([1], False, False)
+    for n in range(half, Z):
+        relay_sibling(n)
+        part = H // (Z - half)
+        attend(list(range(half)), True, False, (n - half) * part, (n - half + 1) * part)
+    for n in range(half, Z):
+        await_sibling(n)
+        score(n)
     loads[5].wait()
-    attend(list(range(2, Z)), False, True)
+    attend(list(range(half, Z)), False, True)
     loads[6].wait()
 
     def project(owner):
@@ -517,7 +517,7 @@
     rope = latent_keys.shape[1] - key_up.shape[2]
     cols = output_weight.shape[1] // mesh.shape["tp"]
     fits = Z > 1 and X == Y == 2 and mesh.shape["tp"] == 4 and R % 16 == 0 and cols % 128 == 0
-    fits = fits and rope * 2 == 128 and (X * Y * C * R) % 128 == 0 and key_up.shape[0] % 8 == 0
+    fits = fits and rope * 2 == 128 and (X * Y * C * R) % 128 == 0 and key_up.shape[0] % 8 == 0 and key_up.shape[0] % (Z - Z // 2) == 0
     return fused(dims, *arrays) if fits else on_device(*arrays)
 
 

time: 36.9 us -> 35 us (0.949)
  Pallas kernels: 36.1 us -> 34.1 us
    pallas_call x1, Pallas kernels: 36.1 us -> 34.1 us  [fused(): pl.pallas_call(partial(fused_kernel, dims, span_len, latent), out_shape=p...]
where the time goes in v2:
time: 35 us; the launch traced here: 34.8 us
  Pallas kernels  34.1 us (97%)
  local copies, waits for them, and re-layouts  0.69 us (2%)
    pallas_call x1, Pallas kernels, fused(): pl.pallas_call(partial(fused_kernel, dims, span_len, latent), out_shape=p...  34.1 us

profile of v2, /device:TPU:0, one launch (start us, length us, event | category | flops | bytes accessed | tf_op | source)
XLA Modules:
  0.0 34.8 jit_solution(10183895910943859973)
XLA Ops:
  0.0 34.1 %shard_map.73 = bf16[128,896]{1,0:T(8,128)(2,1)S(1)} custom-call(s32[16]{0:T(128)} %span_hbm.1, bf16[32,576]{1,0:T(8,128)(2,1)} %own_hbm.1, bf16[128,2048]{1,0:T(8,128)(2,1)} %qp_hbm.1, bf16[128,1024]{1,0:T(8,128)(2,1)} %qr_hbm.1, bf16[16,128,512]{2,1,0:T(8,128)(2,1)} %ku_hbm.1, bf16[16,512,128]{2,1,0:T(8,128)(2,1)} %vu_hbm.1, bf16[2048,3584]{1,0:T(8,128)(2,1)} %w_hbm.1), custom_call_target="tpu_custom_call" | custom-call | tf_op jit(solution)/shard_map/pallas_call | solution.py:473
  34.1 0.7 %copy.9 = bf16[128,896]{1,0:T(8,128)(2,1)} copy(bf16[128,896]{1,0:T(8,128)(2,1)S(1)} %shard_map.73) | data formatting | bytes 458752

commit v3 on v2

--- a/solution.py
+++ b/solution.py
@@ -192,7 +192,7 @@
 def fused_kernel(dims, span_len, latent, span_hbm, own_hbm, qp_hbm, qr_hbm, ku_hbm, vu_hbm, w_hbm,
                  out_ref, span_ref, own_ref, qp, qr, ku, vu, w, keys, queries, bias, scores, acc, top, total,
                  heads_out, own_part, sib_out, sib_in, y_out, y_in,
-                 load_sem, zs, zr, ps, pr, ss, sr, rss, rsr, rys, ryr):
+                 load_sem, plane_sem, line_sem, zs, zr, ps, pr, ss, sr, rss, rsr, rys, ryr):
     Z, X, Y, C = dims
     ctx = lax.axis_index("ctx")
     tp = lax.axis_index("tp")
@@ -224,9 +224,17 @@
     planes = [z] + [z_order(jnp.int32(i)) for i in range(Z - 1)]
 
     barrier = pltpu.get_barrier_semaphore()
-    peers = [z_dev(zz) for zz in planes[1:]] + plane_devs + [sibling]
-    for peer in peers:
-        pl.semaphore_signal(barrier, inc=1, device_id=peer, device_id_type=MESH)
+
+    def on_line(zz):
+        return (zz >= 0) & (zz < Z)
+
+    def greet(semaphore, device):
+        pl.semaphore_signal(semaphore, inc=1, device_id=device, device_id_type=MESH)
+
+    for peer in plane_devs[:2] + [sibling]:
+        greet(barrier, peer)
+    for d in (-1, 1):
+        pl.when(on_line(z + d))(partial(greet, barrier, z_dev(z + d)))
 
     loads = []
     pairs = ((own_hbm, own_ref), (span_hbm, span_ref), (qr_hbm, qr), (qp_hbm, qp), (ku_hbm, ku), (vu_hbm, vu), (w_hbm, w))
@@ -273,45 +281,8 @@
     keys[mine, :latent] = own_ref[:, :latent]
     keys[mine, latent:] = turned
 
-    token = lax.broadcasted_iota(jnp.int32, (T, 1), 0)
-    query_places = jnp.zeros((T, 1), jnp.int32)
-    for n in range(T // span_len):
-        query_places = jnp.where(
-            token // span_len == n, place_of(ctx * T + n * span_len) + lax.rem(token, span_len), query_places
-        )
-    cosine, sine = tables(query_places)
-    first = lane < rope
-    loads[2].wait()
-
-    def turn(n, carry):
-        values = qr[:, pl.ds(pl.multiple_of(n * 128, 128), 128)].astype(jnp.float32)
-        value = rotate(values, cosine, sine) * scale
-        row = pl.multiple_of(2 * n * T, T)
-        queries[pl.ds(row, T), latent:] = jnp.where(first, value, 0.0).astype(jnp.bfloat16)
-        queries[pl.ds(row + T, T), latent:] = jnp.where(first, 0.0, value).astype(jnp.bfloat16)
-        return carry
-
-    lax.fori_loop(0, H // 2, turn, 0)
-    key_lane = lax.broadcasted_iota(jnp.int32, (1, L), 1)
-    for n, plane in enumerate(planes):
-        key_places = jnp.zeros((1, L), jnp.int32)
-        for b in range(L // span_len):
-            start = plane * L + b * span_len
-            key_places = jnp.where(key_lane // span_len == b, place_of(start) + lax.rem(key_lane, span_len), key_places)
-        bias[n] = jnp.where(key_places <= query_places, 0.0, fill_score)
-    loads[3].wait()
-    loads[4].wait()
-
-    def absorb(n, carry):
-        value = jnp.dot(
-            qp[:, pl.ds(pl.multiple_of(n * plain, plain), plain)], ku[n], preferred_element_type=jnp.float32
-        )
-        queries[pl.ds(pl.multiple_of(n * T, T), T), :latent] = (value * scale).astype(jnp.bfloat16)
-        return carry
-
-    lax.fori_loop(0, H, absorb, 0, unroll=4)
-
-    pl.semaphore_wait(barrier, len(peers))
+    ends = on_line(z - 1).astype(jnp.int32) + on_line(z + 1).astype(jnp.int32)
+    pl.semaphore_wait(barrier, 3 + ends)
     sends = []
 
     def send(ref, send_sem, recv_sem, device):
@@ -328,13 +299,13 @@
 
     def send_plane(n):
         ref = rows_at(block(planes[n], x, y, c), R)
-        for kind in (2, 0, 1):
+        for kind in (2, 0, 1) if n > 0 else (0, 1):
             send(ref, ps.at[kind, n], pr.at[kind, planes[n]], plane_devs[kind])
         send_sibling(n, 0)
 
     def relay_plane(n):
         zz = planes[n]
-        arrival(rows_at(block(zz, x, y, c), R), zs.at[n - 1], zr.at[zz], z_dev(zz))
+        arrival(rows_at(block(zz, x, y, c), R), zs.at[zz], zr.at[zz], z_dev(zz))
         send_plane(n)
 
     def relay_sibling(n):
@@ -408,12 +379,72 @@
 
         lax.fori_loop(begin, end, step, 0, unroll=8)
 
-    for n in range(1, Z):
-        send(rows_at(own_row, R), zs.at[n - 1], zr.at[z], z_dev(planes[n]))
+    def own_copy(zz):
+        ref = rows_at(own_row, R)
+        return pltpu.make_async_remote_copy(ref, ref, zs.at[zz], zr.at[z], z_dev(zz), MESH)
+
+    def send_far(k):
+        for n, d in enumerate((-1, 1)):
+            def reach(n=n, d=d):
+                pl.semaphore_wait(line_sem.at[n, k - 2], 1)
+                if k < Z - 1:
+                    pl.when(on_line(z + d))(partial(greet, line_sem.at[n, k - 1], z_dev(z + d)))
+                own_copy(z - d * k).start()
+
+            pl.when(on_line(z - d * k))(reach)
+
+    greet(plane_sem, plane_devs[0])
+    for n, d in enumerate((-1, 1)):
+        pl.when(on_line(z + d) & on_line(z - d))(partial(greet, line_sem.at[n, 0], z_dev(z + d)))
+    for d in (-1, 1):
+        pl.when(on_line(z + d))(lambda d=d: own_copy(z + d).start())
     send_plane(0)
-
+    token = lax.broadcasted_iota(jnp.int32, (T, 1), 0)
+    query_places = jnp.zeros((T, 1), jnp.int32)
+    for n in range(T // span_len):
+        query_places = jnp.where(
+            token // span_len == n, place_of(ctx * T + n * span_len) + lax.rem(token, span_len), query_places
+        )
+    cosine, sine = tables(query_places)
+    first = lane < rope
+    loads[2].wait()
+
+    def turn(n, carry):
+        values = qr[:, pl.ds(pl.multiple_of(n * 128, 128), 128)].astype(jnp.float32)
+        value = rotate(values, cosine, sine) * scale
+        row = pl.multiple_of(2 * n * T, T)
+        queries[pl.ds(row, T), latent:] = jnp.where(first, value, 0.0).astype(jnp.bfloat16)
+        queries[pl.ds(row + T, T), latent:] = jnp.where(first, 0.0, value).astype(jnp.bfloat16)
+        return carry
+
+    lax.fori_loop(0, H // 2, turn, 0)
+    pl.semaphore_wait(plane_sem, 1)
+    send(rows_at(own_row, R), ps.at[2, 0], pr.at[2, z], plane_devs[2])
+    send_far(2)
+    key_lane = lax.broadcasted_iota(jnp.int32, (1, L), 1)
+    for n, plane in enumerate(planes):
+        key_places = jnp.zeros((1, L), jnp.int32)
+        for b in range(L // span_len):
+            start = plane * L + b * span_len
+            key_places = jnp.where(key_lane // span_len == b, place_of(start) + lax.rem(key_lane, span_len), key_places)
+        bias[n] = jnp.where(key_places <= query_places, 0.0, fill_score)
+    for k in range(3, Z):
+        send_far(k)
+    relay_plane(1)
     relay_sibling(0)
-    for n in range(1, Z):
+    loads[3].wait()
+    loads[4].wait()
+
+    def absorb(n, carry):
+        value = jnp.dot(
+            qp[:, pl.ds(pl.multiple_of(n * plain, plain), plain)], ku[n], preferred_element_type=jnp.float32
+        )
+        queries[pl.ds(pl.multiple_of(n * T, T), T), :latent] = (value * scale).astype(jnp.bfloat16)
+        return carry
+
+    lax.fori_loop(0, H, absorb, 0, unroll=4)
+
+    for n in range(2, Z):
         relay_plane(n)
     relay_sibling(1)
     half = Z // 2
@@ -455,6 +486,8 @@
     out_ref[...] = (result + y_in[...].astype(jnp.float32)).astype(out_ref.dtype)
     for copy in sends:
         copy.wait_send()
+    for n in range(1, Z):
+        own_copy(planes[n]).wait_send()
 
 
 def fused(dims, *arrays):
@@ -497,7 +530,8 @@
             pltpu.VMEM((T, cols), bf16),
             pltpu.VMEM((T, cols), bf16),
             dma((7,)),
-            dma((Z - 1,)), dma((Z,)),
+            pltpu.SemaphoreType.REGULAR, pltpu.SemaphoreType.REGULAR((2, Z - 2)),
+            dma((Z,)), dma((Z,)),
             dma((3, Z)), dma((3, Z)),
             dma((Z, 4)), dma((Z, 4)),
             dma((Y,)), dma((Y,)),
@@ -516,7 +550,7 @@
     R, T = latent_keys.shape[0], query_plain.shape[0]
     rope = latent_keys.shape[1] - key_up.shape[2]
     cols = output_weight.shape[1] // mesh.shape["tp"]
-    fits = Z > 1 and X == Y == 2 and mesh.shape["tp"] == 4 and R % 16 == 0 and cols % 128 == 0
+    fits = Z > 2 and X == Y == 2 and mesh.shape["tp"] == 4 and R % 16 == 0 and cols % 128 == 0
     fits = fits and rope * 2 == 128 and (X * Y * C * R) % 128 == 0 and key_up.shape[0] % 8 == 0 and key_up.shape[0] % (Z - Z // 2) == 0
     return fused(dims, *arrays) if fits else on_device(*arrays)
 

time: 35 us -> 33.8 us (0.966)
  Pallas kernels: 34.1 us -> 32.9 us
    pallas_call x1, Pallas kernels: 34.1 us -> 32.9 us  [fused(): pl.pallas_call(partial(fused_kernel, dims, span_len, latent), out_shape=p...]
where the time goes in v3:
time: 33.8 us; the launch traced here: 33.6 us
  Pallas kernels  32.9 us (97%)
  local copies, waits for them, and re-layouts  0.69 us (2%)
    pallas_call x1, Pallas kernels, fused(): pl.pallas_call(partial(fused_kernel, dims, span_len, latent), out_shape=p...  32.9 us
    unnamed x1, local copies, waits for them, and re-layouts  0.69 us

profile of v3, /device:TPU:0, one launch (start us, length us, event | category | flops | bytes accessed | tf_op | source)
XLA Modules:
  0.0 33.6 jit_solution(15879550265544954174)
XLA Ops:
  0.0 32.9 %shard_map.73 = bf16[128,896]{1,0:T(8,128)(2,1)S(1)} custom-call(s32[16]{0:T(128)} %span_hbm.1, bf16[32,576]{1,0:T(8,128)(2,1)} %own_hbm.1, bf16[128,2048]{1,0:T(8,128)(2,1)} %qp_hbm.1, bf16[128,1024]{1,0:T(8,128)(2,1)} %qr_hbm.1, bf16[16,128,512]{2,1,0:T(8,128)(2,1)} %ku_hbm.1, bf16[16,512,128]{2,1,0:T(8,128)(2,1)} %vu_hbm.1, bf16[2048,3584]{1,0:T(8,128)(2,1)} %w_hbm.1), custom_call_target="tpu_custom_call" | custom-call | tf_op jit(solution)/shard_map/pallas_call | solution.py:506
  32.9 0.7 %copy.9 = bf16[128,896]{1,0:T(8,128)(2,1)} copy(bf16[128,896]{1,0:T(8,128)(2,1)S(1)} %shard_map.73) | data formatting | bytes 458752

commit v4 on v3

--- a/solution.py
+++ b/solution.py
@@ -462,28 +462,50 @@
     attend(list(range(half, Z)), False, True)
     loads[6].wait()
 
-    def project(owner):
+    split = (cols // 256 + 1) // 2 * 256
+    spans = ((0, split), (split, cols - split))
+
+    def project(owner, begin, size):
         return jnp.dot(
-            heads_out[...], w[:, pl.ds(pl.multiple_of(owner * cols, 128), cols)],
+            heads_out[...], w[:, pl.ds(pl.multiple_of(owner * cols + begin, 128), size)],
             preferred_element_type=jnp.float32,
         )
 
+    def sibling_copy(j, n):
+        part = pl.ds(spans[n][0], spans[n][1])
+        return pltpu.make_async_remote_copy(
+            sib_out.at[j, :, part], sib_in.at[j, :, part], rss.at[j, n], rsr.at[j, n], sibling, MESH
+        )
+
+    def peer_copy(n):
+        part = pl.ds(spans[n][0], spans[n][1])
+        return pltpu.make_async_remote_copy(y_out.at[:, part], y_in.at[:, part], rys.at[n], ryr.at[n], y_peer, MESH)
+
     for j in (1, 0):
         target = lax.rem(y + j, Y) * C
-        sib_out[j] = project(target + C - 1 - c).astype(jnp.bfloat16)
-        copy = pltpu.make_async_remote_copy(sib_out.at[j], sib_in.at[j], rss.at[j], rsr.at[j], sibling, MESH)
-        copy.start()
-        own_part[...] = project(target + c)
-        copy.wait_recv()
-        sends.append(copy)
-        if j > 0:
-            y_out[...] = (own_part[...] + sib_in[j].astype(jnp.float32)).astype(jnp.bfloat16)
-            y_copy = pltpu.make_async_remote_copy(y_out, y_in, rys.at[0], ryr.at[0], y_peer, MESH)
-            y_copy.start()
-            sends.append(y_copy)
-    result = own_part[...] + sib_in[0].astype(jnp.float32)
-    y_copy.wait_recv()
-    out_ref[...] = (result + y_in[...].astype(jnp.float32)).astype(out_ref.dtype)
+        for n, (begin, size) in enumerate(spans):
+            sib_out[j, :, begin:begin + size] = project(target + C - 1 - c, begin, size).astype(jnp.bfloat16)
+            copy = sibling_copy(j, n)
+            copy.start()
+            sends.append(copy)
+        for n, (begin, size) in enumerate(spans):
+            part = project(target + c, begin, size)
+            if j > 0:
+                sibling_copy(j, n).wait_recv()
+                part = part + sib_in[j, :, begin:begin + size].astype(jnp.float32)
+                y_out[:, begin:begin + size] = part.astype(jnp.bfloat16)
+                copy = peer_copy(n)
+                copy.start()
+                sends.append(copy)
+            else:
+                own_part[:, begin:begin + size] = part
+    for n, (begin, size) in enumerate(spans):
+        sibling_copy(0, n).wait_recv()
+        own_part[:, begin:begin + size] += sib_in[0, :, begin:begin + size].astype(jnp.float32)
+    for n, (begin, size) in enumerate(spans):
+        peer_copy(n).wait_recv()
+        whole = own_part[:, begin:begin + size] + y_in[:, begin:begin + size].astype(jnp.float32)
+        out_ref[:, begin:begin + size] = whole.astype(out_ref.dtype)
     for copy in sends:
         copy.wait_send()
     for n in range(1, Z):
@@ -534,8 +556,8 @@
             dma((Z,)), dma((Z,)),
             dma((3, Z)), dma((3, Z)),
             dma((Z, 4)), dma((Z, 4)),
-            dma((Y,)), dma((Y,)),
-            dma((1,)), dma((1,)),
+            dma((Y, 2)), dma((Y, 2)),
+            dma((2,)), dma((2,)),
         ],
         compiler_params=pltpu.CompilerParams(
             collective_id=0, has_side_effects=True, vmem_limit_bytes=56 * 1024 * 1024
@@ -550,7 +572,7 @@
     R, T = latent_keys.shape[0], query_plain.shape[0]
     rope = latent_keys.shape[1] - key_up.shape[2]
     cols = output_weight.shape[1] // mesh.shape["tp"]
-    fits = Z > 2 and X == Y == 2 and mesh.shape["tp"] == 4 and R % 16 == 0 and cols % 128 == 0
+    fits = Z > 2 and X == Y == 2 and mesh.shape["tp"] == 4 and R % 16 == 0 and cols % 128 == 0 and cols > 256
     fits = fits and rope * 2 == 128 and (X * Y * C * R) % 128 == 0 and key_up.shape[0] % 8 == 0 and key_up.shape[0] % (Z - Z // 2) == 0
     return fused(dims, *arrays) if fits else on_device(*arrays)
 

time: 33.8 us -> 33.8 us (level)
  no operation moved by 1% of the time
where the time goes in v4:
time: 33.8 us; the launch traced here: 33.7 us
  Pallas kernels  33 us (98%)
  local copies, waits for them, and re-layouts  0.69 us (2%)
    pallas_call x1, Pallas kernels, fused(): pl.pallas_call(partial(fused_kernel, dims, span_len, latent), out_shape=p...  33 us
    unnamed x1, local copies, waits for them, and re-layouts  0.69 us

profile of v4, /device:TPU:0, one launch (start us, length us, event | category | flops | bytes accessed | tf_op | source)
XLA Modules:
  0.0 33.7 jit_solution(12232114525379534703)
XLA Ops:
  0.0 33.0 %shard_map.73 = bf16[128,896]{1,0:T(8,128)(2,1)S(1)} custom-call(s32[16]{0:T(128)} %span_hbm.1, bf16[32,576]{1,0:T(8,128)(2,1)} %own_hbm.1, bf16[128,2048]{1,0:T(8,128)(2,1)} %qp_hbm.1, bf16[128,1024]{1,0:T(8,128)(2,1)} %qr_hbm.1, bf16[16,128,512]{2,1,0:T(8,128)(2,1)} %ku_hbm.1, bf16[16,512,128]{2,1,0:T(8,128)(2,1)} %vu_hbm.1, bf16[2048,3584]{1,0:T(8,128)(2,1)} %w_hbm.1), custom_call_target="tpu_custom_call" | custom-call | tf_op jit(solution)/shard_map/pallas_call | solution.py:528
  33.0 0.7 %copy.9 = bf16[128,896]{1,0:T(8,128)(2,1)} copy(bf16[128,896]{1,0:T(8,128)(2,1)S(1)} %shard_map.73) | data formatting | bytes 458752
